TPU v7x, 32 devices: a whole 2x2x4 slice. The times are simulated.
32 devices in a mesh: shard: 2 (over core), ctx: 4 (over y, x), tp: 4 (over z).
Axes of the slice: x: 2, y: 2, z: 4, core: 2. Of those that a mesh axis runs over, the one named last changes fastest.
Arguments:
- layer_input: bfloat16 [8, 1024, 2048], P('shard', 'ctx'), may hold values from -6 to 6
- output_gradient: bfloat16 [8, 1024, 2048], P('shard', 'ctx'), may hold values from -6 to 6
- picture_piece_starts: int32 [8, 2], P('shard'), may hold values from 0 to 768, as said below
- sequence_adapter_index: int32 [8], P('shard'), may hold values from 0 to 7
- attention_norm_gain: float32 [2048], replicated, may hold values from 0.5 to 1.5
- attention_norm_bias: float32 [2048], replicated, may hold values from -1 to 1
- feedforward_norm_gain: float32 [2048], replicated, may hold values from 0.5 to 1.5
- feedforward_norm_bias: float32 [2048], replicated, may hold values from -1 to 1
- query_key_value_weight: bfloat16 [2048, 3, 2048], P('shard', None, 'tp'), may hold values from -0.125 to 0.125
- attention_output_weight: bfloat16 [2048, 2048], P('tp', 'shard'), may hold values from -0.375 to 0.375
- up_projection_weight: bfloat16 [2048, 8192], P('shard', 'tp'), may hold values from -0.125 to 0.125
- down_projection_weight: bfloat16 [8192, 2048], P('tp', 'shard'), may hold values from -0.09375 to 0.09375
- adapter_projection_first: bfloat16 [8, 2048, 16], replicated, may hold values from -0.125 to 0.125
- adapter_projection_second: bfloat16 [8, 16, 3, 2048], P(None, None, None, 'tp'), may hold values from -0.75 to 0.75
- adapter_heads_first: bfloat16 [8, 2048, 16], P(None, 'tp'), may hold values from -0.375 to 0.375
- adapter_heads_second: bfloat16 [8, 16, 2048], replicated, may hold values from -0.75 to 0.75
- adapter_up_first: bfloat16 [8, 2048, 16], replicated, may hold values from -0.125 to 0.125
- adapter_up_second: bfloat16 [8, 16, 8192], P(None, None, 'tp'), may hold values from -0.75 to 0.75
- adapter_down_first: bfloat16 [8, 8192, 16], P(None, 'tp'), may hold values from -0.09375 to 0.09375
- adapter_down_second: bfloat16 [8, 16, 2048], replicated, may hold values from -0.75 to 0.75
Outputs:
- layer_out: bfloat16 [8, 1024, 2048], P('shard', 'ctx')
- input_grad: bfloat16 [8, 1024, 2048], P('shard', 'ctx')
- qkv_in_grad: float32 [8, 2048, 16], replicated
- qkv_out_grad: float32 [8, 16, 3, 2048], P(None, None, None, 'tp')
- heads_in_grad: float32 [8, 2048, 16], P(None, 'tp')
- heads_out_grad: float32 [8, 16, 2048], replicated
- up_in_grad: float32 [8, 2048, 16], replicated
- up_out_grad: float32 [8, 16, 8192], P(None, None, 'tp')
- down_in_grad: float32 [8, 8192, 16], P(None, 'tp')
- down_out_grad: float32 [8, 16, 2048], replicated
Inputs may be any that keep to these rules, and one draw needn't show every extreme that they name: `picture_piece_starts`: piece c of a sequence starts within positions c * 512 to (c + 1) * 512 - 256, so pieces never meet; in some sequence a piece starts at 0, in some sequence a piece ends at 1024.
All inputs are finite; a program needn't handle non-finite values.
Results may differ from a plain program's by a relative error of at most 0.019.
Values may be sent and summed in bfloat16 or wider, within the bound.
A program may use at most 320 MiB of HBM per device.

v0:
```python
import jax
import jax.numpy as jnp
from jax import lax
from jax.sharding import PartitionSpec as P

HD = 128
PIC = 256
NORM_EPS = 1e-05


def layer_norm(inputs, gains, biases):
    average = jnp.mean(inputs, axis=-1, keepdims=True)
    centred = inputs - average
    spread = jnp.mean(centred * centred, axis=-1, keepdims=True)
    return centred * lax.rsqrt(spread + NORM_EPS) * gains + biases


def gelu_tanh(inputs):
    return (
        0.5
        * inputs
        * (1.0 + jnp.tanh(0.7978845608028654 * (inputs + 0.044715 * inputs * inputs * inputs)))
    )


def flattened_first(adapter_mat):
    adapter_tables, inner_dim, rank_width = adapter_mat.shape
    return jnp.transpose(adapter_mat, (1, 0, 2)).reshape(inner_dim, adapter_tables * rank_width)


def flattened_second(adapter_mat):
    return adapter_mat.reshape(adapter_mat.shape[0] * adapter_mat.shape[1], -1)


def unflat_in(grad_flat, adapter_tables):
    inner_dim = grad_flat.shape[0]
    return jnp.transpose(grad_flat.reshape(inner_dim, adapter_tables, -1), (1, 0, 2))


def matmul(left_mat, right_mat):
    return jnp.dot(left_mat, right_mat, preferred_element_type=jnp.float32)


def matmul_tn(left_mat, right_mat):
    return lax.dot_general(
        left_mat, right_mat, (((0,), (0,)), ((), ())), preferred_element_type=jnp.float32
    )


def matmul_nt(left_mat, right_mat):
    return lax.dot_general(
        left_mat, right_mat, (((1,), (1,)), ((), ())), preferred_element_type=jnp.float32
    )


def piece_labels(starts, positions):
    inside = (positions[None, None, :] >= starts[:, :, None]) & (
        positions[None, None, :] < starts[:, :, None] + PIC
    )
    labels = jnp.arange(1, starts.shape[1] + 1, dtype=jnp.int32)
    return jnp.sum(jnp.where(inside, labels[None, :, None], 0), axis=1)


def visible(query_pos, key_pos, query_labels, key_labels):
    causal = key_pos[None, None, :] <= query_pos[None, :, None]
    shared = (query_labels[:, :, None] == key_labels[:, None, :]) & (query_labels[:, :, None] > 0)
    return causal | shared


def exponents(queries, key_rows, query_pos, key_pos, visible_mask, slopes):
    score_scale = queries.shape[-1] ** (-0.5)
    logits = (
        jnp.einsum("sqhd,skhd->shqk", queries, key_rows, preferred_element_type=jnp.float32)
        * score_scale
    )
    distance = jnp.abs(query_pos[:, None] - key_pos[None, :]).astype(jnp.float32)
    logits = logits - slopes[None, :, None, None] * distance[None, None]
    return jnp.where(visible_mask[:, None], jnp.exp(logits), 0.0)


def block_grads(
    queries, scaled_grad, row_delta, key_rows, value_rows, query_pos, key_pos, visible_mask, slopes
):
    score_scale = queries.shape[-1] ** (-0.5)
    exponent = exponents(queries, key_rows, query_pos, key_pos, visible_mask, slopes)
    products_gv = jnp.einsum(
        "sqhd,skhd->shqk", scaled_grad, value_rows, preferred_element_type=jnp.float32
    )
    grad_logits = (
        exponent * (products_gv - jnp.transpose(row_delta, (0, 2, 1))[..., None])
    ).astype(jnp.bfloat16)
    grad_queries = (
        jnp.einsum("shqk,skhd->sqhd", grad_logits, key_rows, preferred_element_type=jnp.float32)
        * score_scale
    )
    grad_keyrows = (
        jnp.einsum("shqk,sqhd->skhd", grad_logits, queries, preferred_element_type=jnp.float32)
        * score_scale
    )
    grad_valrows = jnp.einsum(
        "shqk,sqhd->skhd",
        exponent.astype(jnp.bfloat16),
        scaled_grad,
        preferred_element_type=jnp.float32,
    )
    return (grad_queries, grad_keyrows, grad_valrows)


def reduce_heads(partials):
    return lax.psum((partials[0], partials[1]), "tp")


def body(
    layer_input,
    output_gradient,
    picture_piece_starts,
    sequence_adapter_index,
    attention_norm_gain,
    attention_norm_bias,
    feedforward_norm_gain,
    feedforward_norm_bias,
    query_key_value_weight,
    attention_output_weight,
    up_projection_weight,
    down_projection_weight,
    adapter_projection_first,
    adapter_projection_second,
    adapter_heads_first,
    adapter_heads_second,
    adapter_up_first,
    adapter_up_second,
    adapter_down_first,
    adapter_down_second,
):
    seq_here, local_len, model_width = layer_input.shape
    tok_rows = seq_here * local_len
    adapter_tables = adapter_projection_first.shape[0]
    rank_width = adapter_projection_first.shape[2]
    head_width = HD
    device_heads = adapter_projection_second.shape[-1] // head_width
    local_width = device_heads * head_width
    columns = jnp.arange(adapter_tables * rank_width, dtype=jnp.int32) // rank_width
    chosen = (sequence_adapter_index[:, None] == columns[None, :]).astype(jnp.float32)
    select = jnp.broadcast_to(
        chosen[:, None, :], (seq_here, local_len, adapter_tables * rank_width)
    ).reshape(tok_rows, adapter_tables * rank_width)
    head_ids = lax.axis_index("tp") * device_heads + jnp.arange(device_heads, dtype=jnp.int32)
    slopes = jnp.exp2(
        -8.0 * (head_ids.astype(jnp.float32) + 1.0) / (device_heads * lax.axis_size("tp"))
    )
    here_pos = lax.axis_index("ctx") * local_len + jnp.arange(local_len, dtype=jnp.int32)
    here_labels = piece_labels(picture_piece_starts, here_pos)
    projection_first_flattened = flattened_first(adapter_projection_first)
    projection_second_flattened = flattened_second(adapter_projection_second)
    heads_first_flattened = flattened_first(adapter_heads_first)
    heads_second_flattened = flattened_second(adapter_heads_second)
    up_first_flattened = flattened_first(adapter_up_first)
    up_second_flattened = flattened_second(adapter_up_second)
    down_first_flattened = flattened_first(adapter_down_first)
    down_second_flattened = flattened_second(adapter_down_second)
    residual = layer_input.reshape(tok_rows, model_width).astype(jnp.float32)
    first_norm, first_back_full = jax.vjp(
        lambda inputs: layer_norm(inputs, attention_norm_gain, attention_norm_bias), residual
    )
    first_act = first_norm.astype(jnp.bfloat16)
    gathered_rows = (
        lax.all_gather(query_key_value_weight, "shard", axis=0, tiled=True),
        lax.all_gather(up_projection_weight, "shard", axis=0, tiled=True),
    )
    qkv_full = gathered_rows[0].reshape(model_width, 3 * local_width)
    up_full = gathered_rows[1]
    gathered_cols = (
        lax.all_gather(attention_output_weight, "shard", axis=1, tiled=True),
        lax.all_gather(down_projection_weight, "shard", axis=1, tiled=True),
    )
    heads_full = gathered_cols[0]
    down_full = gathered_cols[1]
    first_low = (matmul(first_act, projection_first_flattened) * select).astype(jnp.bfloat16)
    projected = (
        matmul(first_act, qkv_full) + matmul(first_low, projection_second_flattened)
    ).astype(jnp.bfloat16)
    queries_flat = projected[:, :local_width].reshape(seq_here, local_len, local_width)
    queries = queries_flat.reshape(seq_here, local_len, device_heads, head_width)
    key_rows = projected[:, local_width : 2 * local_width].reshape(seq_here, local_len, local_width)
    value_rows = projected[:, 2 * local_width :].reshape(seq_here, local_len, local_width)
    pieces = (
        lax.all_gather(key_rows, "ctx", axis=1, tiled=True),
        lax.all_gather(value_rows, "ctx", axis=1, tiled=True),
    )
    piece_len = pieces[0].shape[1]
    key_pos = jnp.arange(piece_len, dtype=jnp.int32)
    key_labels = piece_labels(picture_piece_starts, key_pos)
    visible_mask = visible(here_pos, key_pos, here_labels, key_labels)
    piece_keys = pieces[0].reshape(seq_here, piece_len, device_heads, head_width)
    piece_values = pieces[1].reshape(seq_here, piece_len, device_heads, head_width)
    exponent = exponents(queries, piece_keys, here_pos, key_pos, visible_mask, slopes)
    weighted = jnp.einsum(
        "shqk,skhd->sqhd",
        exponent.astype(jnp.bfloat16),
        piece_values,
        preferred_element_type=jnp.float32,
    )
    weighted, totals = (weighted, jnp.sum(exponent, axis=-1))
    per_total = jnp.transpose(totals, (0, 2, 1))[..., None]
    heads_raw = weighted / per_total
    heads_act = heads_raw.reshape(tok_rows, local_width).astype(jnp.bfloat16)
    heads_part = matmul(heads_act, heads_full)
    heads_low_part = matmul(heads_act, heads_first_flattened)
    attn_total, attn_low_total = reduce_heads((heads_part, heads_low_part))
    heads_low_here = (attn_low_total * select).astype(jnp.bfloat16)
    middle_here = residual + attn_total + matmul(heads_low_here, heads_second_flattened)
    second_norm, second_back = jax.vjp(
        lambda inputs: layer_norm(inputs, feedforward_norm_gain, feedforward_norm_bias), middle_here
    )
    second_act_here = second_norm.astype(jnp.bfloat16)
    up_low_here = (matmul(second_act_here, up_first_flattened) * select).astype(jnp.bfloat16)
    second_act, up_low, heads_low = (second_act_here, up_low_here, heads_low_here)
    hidden = matmul(second_act, up_full) + matmul(up_low, up_second_flattened)
    activated, gelu_back = jax.vjp(gelu_tanh, hidden)
    activated = activated.astype(jnp.bfloat16)
    down_part = matmul(activated, down_full)
    down_low_part = matmul(activated, down_first_flattened)
    ffn_total, ffn_low_total = reduce_heads((down_part, down_low_part))
    down_low_here = (ffn_low_total * select).astype(jnp.bfloat16)
    result_here = (middle_here + ffn_total + matmul(down_low_here, down_second_flattened)).astype(
        jnp.bfloat16
    )
    grad_top_low = output_gradient.reshape(tok_rows, model_width)
    grad_top = grad_top_low.astype(jnp.float32)
    down_back = (matmul_nt(grad_top_low, down_second_flattened) * select).astype(jnp.bfloat16)
    grad_down_in = matmul_tn(activated, down_back)
    grad_activated = matmul_nt(grad_top_low, down_full) + matmul_nt(down_back, down_first_flattened)
    grad_hidden = gelu_back(grad_activated)[0].astype(jnp.bfloat16)
    up_second_gradient = matmul_tn(up_low, grad_hidden)
    ffn_back_part = matmul_nt(grad_hidden, up_full)
    ffn_back_low = matmul_nt(grad_hidden, up_second_flattened)
    back_total, back_low_total = reduce_heads((ffn_back_part, ffn_back_low))
    up_back_here = (back_low_total * select).astype(jnp.bfloat16)
    grad_second = back_total + matmul_nt(up_back_here, up_first_flattened)
    grad_middle_here = grad_top + second_back(grad_second)[0]
    grad_middle_low_here = grad_middle_here.astype(jnp.bfloat16)
    heads_back_here = (matmul_nt(grad_middle_low_here, heads_second_flattened) * select).astype(
        jnp.bfloat16
    )
    result_rows, down_low, grad_middle_low, heads_back, up_back = (
        result_here,
        down_low_here,
        grad_middle_low_here,
        heads_back_here,
        up_back_here,
    )
    layer_out = result_rows.reshape(layer_input.shape)
    down_second_gradient = matmul_tn(down_low, grad_top_low)
    grad_up_in = matmul_tn(second_act, up_back)
    heads_second_gradient = matmul_tn(heads_low, grad_middle_low)
    grad_heads_in = matmul_tn(heads_act, heads_back)
    grad_heads = (
        matmul_nt(grad_middle_low, heads_full) + matmul_nt(heads_back, heads_first_flattened)
    ).astype(jnp.bfloat16)
    grad_heads_wide = grad_heads.reshape(seq_here, local_len, device_heads, head_width).astype(
        jnp.float32
    )
    scaled_grad = (grad_heads_wide / per_total).astype(jnp.bfloat16)
    row_delta = jnp.sum(grad_heads_wide * heads_raw, axis=-1) / per_total[..., 0]
    pieces = (
        lax.all_gather(key_rows, "ctx", axis=1, tiled=True),
        lax.all_gather(value_rows, "ctx", axis=1, tiled=True),
    )
    piece_len = pieces[0].shape[1]
    key_pos = jnp.arange(piece_len, dtype=jnp.int32)
    key_labels = piece_labels(picture_piece_starts, key_pos)
    visible_mask = visible(here_pos, key_pos, here_labels, key_labels)
    piece_keys = pieces[0].reshape(seq_here, piece_len, device_heads, head_width)
    piece_values = pieces[1].reshape(seq_here, piece_len, device_heads, head_width)
    grad_queries, grad_keyrows, grad_valrows = block_grads(
        queries,
        scaled_grad,
        row_delta,
        piece_keys,
        piece_values,
        here_pos,
        key_pos,
        visible_mask,
        slopes,
    )
    grad_keys_all, grad_values_all = (
        lax.psum_scatter(grad_keyrows, "ctx", scatter_dimension=1, tiled=True),
        lax.psum_scatter(grad_valrows, "ctx", scatter_dimension=1, tiled=True),
    )
    grad_projected = jnp.concatenate(
        [
            grad_queries.reshape(tok_rows, local_width),
            grad_keys_all.reshape(tok_rows, local_width),
            grad_values_all.reshape(tok_rows, local_width),
        ],
        axis=1,
    ).astype(jnp.bfloat16)
    projection_second_gradient = matmul_tn(first_low, grad_projected)
    attn_back_part = matmul_nt(grad_projected, qkv_full)
    attn_back_low = matmul_nt(grad_projected, projection_second_flattened)
    first_total, first_low_total = reduce_heads((attn_back_part, attn_back_low))
    qkv_back_here = (first_low_total * select).astype(jnp.bfloat16)
    grad_first = first_total + matmul_nt(qkv_back_here, projection_first_flattened)
    input_here = (grad_middle_here + first_back_full(grad_first)[0]).astype(jnp.bfloat16)
    input_rows, qkv_back = (input_here, qkv_back_here)
    input_grad = input_rows.reshape(layer_input.shape)
    grad_qkv_in = matmul_tn(first_act, qkv_back)
    adapter_terms = (
        unflat_in(grad_qkv_in, adapter_tables),
        projection_second_gradient.reshape(adapter_projection_second.shape),
        unflat_in(grad_heads_in, adapter_tables),
        heads_second_gradient.reshape(adapter_heads_second.shape),
        unflat_in(grad_up_in, adapter_tables),
        up_second_gradient.reshape(adapter_up_second.shape),
        unflat_in(grad_down_in, adapter_tables),
        down_second_gradient.reshape(adapter_down_second.shape),
    )
    summed = lax.psum(
        (
            adapter_terms[0],
            adapter_terms[1],
            adapter_terms[2],
            adapter_terms[3],
            adapter_terms[4],
            adapter_terms[5],
            adapter_terms[6],
            adapter_terms[7],
        ),
        ("shard", "ctx"),
    )
    return (
        layer_out,
        input_grad,
        summed[0],
        summed[1],
        summed[2],
        summed[3],
        summed[4],
        summed[5],
        summed[6],
        summed[7],
    )


def solution(mesh):
    placed = (
        P("shard", "ctx", None),
        P("shard", "ctx", None),
        P("shard", None),
        P("shard"),
        P(),
        P(),
        P(),
        P(),
        P("shard", None, "tp"),
        P("tp", "shard"),
        P("shard", "tp"),
        P("tp", "shard"),
        P(),
        P(None, None, None, "tp"),
        P(None, "tp", None),
        P(),
        P(),
        P(None, None, "tp"),
        P(None, "tp", None),
        P(),
    )
    return jax.shard_map(
        body,
        mesh=mesh,
        in_specs=placed,
        out_specs=(
            P("shard", "ctx", None),
            P("shard", "ctx", None),
            P(),
            P(None, None, None, "tp"),
            P(None, "tp", None),
            P(),
            P(),
            P(None, None, "tp"),
            P(None, "tp", None),
            P(),
        ),
        check_vma=False,
    )
```

profile of v0, /device:TPU:0, one launch (start us, length us, event | category | flops | bytes accessed | tf_op | source)
XLA Modules:
  0.0 1857.7 jit_solution(7738910371380799832)
XLA Ops:
  7.3 4.7 copy.69
  12.6 3.2 convert_reduce_fusion
  23.4 8.2 all-gather.7.cloned.1.call-done
  31.6 10.1 fusion.54
  47.8 2.6 broadcast_multiply_fusion
  54.1 43.8 %all-gather.9.cloned.1.call-done = bf16[4,1024,512]{2,1,0:T(8,128)(2,1)} async-done(((bf16[4,256,512]{2,1,0:T(8,128)(2,1)}), bf16[4,1024,512]{2,1,0:T(8,128)(2,1)}) %all-gather.9.cloned.1.call-update) | async-done | bytes 4194320 | tf_op jit(solution)/shard_map/all_gather | solution.py:188
  97.9 6.3 copy.71
  104.2 48.5 %all-gather.11.cloned.1.call-done = bf16[4,1024,512]{1,2,0:T(8,128)(2,1)} async-done(((bf16[4,256,512]{1,2,0:T(8,128)(2,1)}), bf16[4,1024,512]{1,2,0:T(8,128)(2,1)}) %all-gather.11.cloned.1.call-update) | async-done | bytes 4194320 | tf_op jit(solution)/shard_map/all_gather | solution.py:187
  152.8 12.5 fusion.51
  165.3 10.2 fusion.52
  177.4 7.6 fusion.34
  186.1 3.4 fusion.30
  189.6 14.8 fusion.58
  204.4 294.8 %all-reduce.15.cloned.1.call-done = (f32[1024,2048]{1,0:T(8,128)}, f32[1024,128]{1,0:T(8,128)}) async-done(((f32[1024,2048]{1,0:T(8,128)}, f32[1024,128]{1,0:T(8,128)}), (f32[1024,2048]{1,0:T(8,128)}, f32[1024,128]{1,0:T(8,128)})) %all-reduce.15.cloned.1.call-update) | async-done | bytes 8912912 | tf_op jit(solution)/shard_map/psum | solution.py:110
  500.3 6.3 fusion.53
  514.4 5.2 all-gather.15.cloned.1.call-done
  519.6 12.5 fusion.55
  532.1 4.9 multiply_convert_fusion.1
  537.0 9.4 fusion.3
  548.6 11.2 fusion.59
  559.8 309.0 %all-reduce.13.cloned.1.call-done = (f32[1024,2048]{1,0:T(8,128)}, f32[1024,128]{1,0:T(8,128)}) async-done(((f32[1024,2048]{1,0:T(8,128)}, f32[1024,128]{1,0:T(8,128)}), (f32[1024,2048]{1,0:T(8,128)}, f32[1024,128]{1,0:T(8,128)})) %all-reduce.13.cloned.1.call-update) | async-done | bytes 8912912 | tf_op jit(solution)/shard_map/psum | solution.py:110
  869.9 7.4 multiply_reduce_fusion
  877.4 4.8 fusion.48
  882.2 3.6 fusion.16
  886.8 3.4 fusion.31
  890.3 5.2 fusion.61
  901.5 8.6 multiply_convert_fusion
  910.1 3.2 copy-done.9
  913.3 4.9 multiply_bitcast_fusion
  918.4 10.6 fusion.21
  930.1 4.5 fusion.57
  934.6 14.9 fusion.56
  949.5 2.9 fusion.27
  954.3 49.3 %reduce-scatter.3.cloned.1.call-done = f32[4,256,4,128]{1,3,2,0:T(8,128)} async-done(((f32[4,1024,4,128]{1,3,2,0:T(8,128)}), f32[4,256,4,128]{1,3,2,0:T(8,128)}) %reduce-scatter.3.cloned.1.call-update) | async-done | bytes 2097168 | tf_op jit(solution)/shard_map/reduce_scatter | solution.py:287
  1006.1 86.9 %reduce-scatter.5.cloned.1.call-done = f32[4,256,4,128]{1,3,2,0:T(8,128)} async-done(((f32[4,1024,4,128]{1,3,2,0:T(8,128)}), f32[4,256,4,128]{1,3,2,0:T(8,128)}) %reduce-scatter.5.cloned.1.call-update) | async-done | bytes 2097168 | tf_op jit(solution)/shard_map/reduce_scatter | solution.py:288
  1099.7 3.6 fusion.63
  1103.3 11.8 fusion.62
  1116.7 3.9 fusion.67
  1120.7 4.5 fusion.68
  1126.3 4.2 fusion.66
  1132.3 2.6 fusion.64
  1136.4 575.2 %all-reduce.11.cloned.1.call-done = (f32[1024,2048]{1,0:T(8,128)}, f32[1024,128]{1,0:T(8,128)}, f32[1024,2048]{1,0:T(8,128)}, f32[1024,128]{1,0:T(8,128)}) async-done(((f32[1024,2048]{1,0:T(8,128)}, f32[1024,128]{1,0:T(8,128)}, f32[1024,2048]{1,0:T(8,128)}, f32[1024,128]{1,0:T(8,128)}), (f32[1024,2048]{1,0:T(8,128)}, f32[1024,128]{1,0:T(8,128)}, f32[1024,2048]{1,0:T(8,128)}, ...) | async-done | bytes 17825808 | tf_op jit(solution)/shard_map/psum | solution.py:110
  1713.2 4.0 convolution_bitcast_fusion
  1719.1 8.5 fusion.10
  1728.4 5.8 fusion.47
  1734.2 7.1 add_convert_fusion.1
  1741.4 7.2 add_convert_fusion
  1748.6 88.1 %all-reduce.9.cloned.1.call-done = (f32[8,2048,16]{1,2,0:T(8,128)}, f32[8,16,3,512]{3,2,1,0:T(4,128)}, f32[8,512,16]{1,2,0:T(8,128)}, f32[8,16,2048]{2,1,0:T(8,1...) async-done(((f32[8,2048,16]{1,2,0:T(8,128)}, f32[8,16,3,512]{3,2,1,0:T(4,128)}, ...) | async-done | bytes 7340048 | tf_op jit(solution)/shard_map/psum | solution.py:318
  (223 shorter events, 76.2 us)
Async XLA Ops:
  7.2 524.9 %copy-start = (bf16[8,16,2048]{2,1,0:T(8,128)(2,1)S(1)}, bf16[8,16,2048]{2,1,0:T(8,128)(2,1)}, u32[]{:S(2)}) copy-start(bf16[8,16,2048]{2,1,0:T(8,128)(2,1)} %param.37) | copy-start | bytes 1572868
  7.2 11.1 copy-start.45
  7.2 11.1 copy-start.51
  7.2 24.4 %all-gather.7.cloned.1.call-start = ((), (), s32[]{:S(2)}) async-start(), calls=%async_computation.2 | async-start | bytes 9437184 | tf_op jit(solution)/shard_map/all_gather | solution.py:167
  12.0 85.9 %all-gather.9.cloned.1.call-start = ((), (), s32[]{:S(2)}) async-start(), calls=%async_computation.3 | async-start | bytes 5242880 | tf_op jit(solution)/shard_map/all_gather | solution.py:188
  12.5 29.2 %copy-start.20 = (bf16[16,8,3,512]{3,1,2,0:T(8,128)(2,1)}, bf16[16,8,3,512]{3,1,2,0:T(8,128)(2,1)S(1)}, u32[]{:S(2)}) copy-start(bf16[16,8,3,512]{3,1,2,0:T(8,128)(2,1)S(1)} %copy.93) | copy-start | bytes 1179652
  12.6 856.2 %copy-start.40 = (f32[4,128]{1,0:T(4,128)}, f32[4,128]{1,0:T(4,128)S(1)}, u32[]{:S(2)}) copy-start(f32[4,128]{1,0:T(4,128)S(1)} %compare_convert_fusion) | copy-start | bytes 6148
  12.6 9.5 copy-start.28
  23.4 18.3 copy-start.24
  44.0 108.8 %all-gather.11.cloned.1.call-start = ((), (), s32[]{:S(2)}) async-start(), calls=%async_computation.4 | async-start | bytes 5242880 | tf_op jit(solution)/shard_map/all_gather | solution.py:187
  45.4 132.1 %all-gather.13.cloned.1.call-start = ((), (), s32[]{:S(2)}) async-start(), calls=%async_computation.5 | async-start | bytes 3145728 | tf_op jit(solution)/shard_map/all_gather | solution.py:173
  45.9 143.6 %all-gather.17.cloned.1.call-start = ((), (), s32[]{:S(2)}) async-start(), calls=%async_computation.7 | async-start | bytes 12582912 | tf_op jit(solution)/shard_map/all_gather | solution.py:174
  46.5 452.7 %all-reduce.15.cloned.1.call-start = ((), (), s32[]{:S(2)}) async-start(), calls=%async_computation.13 | async-start | bytes 17825792 | tf_op jit(solution)/shard_map/psum | solution.py:110
  54.1 111.2 %copy-start.16 = (bf16[4,256,4,128]{1,3,2,0:T(8,128)(2,1)}, bf16[4,256,4,128]{1,3,2,0:T(8,128)(2,1)S(1)}, u32[]{:S(2)}) copy-start(bf16[4,256,4,128]{1,3,2,0:T(8,128)(2,1)S(1)} %copy.82) | copy-start | bytes 3145732
  152.8 12.5 copy-start.10
  165.3 10.9 copy-start.38
  176.2 8.9 copy-start.18
  185.1 334.5 %all-gather.15.cloned.1.call-start = ((), (), s32[]{:S(2)}) async-start(), calls=%async_computation.6 | async-start | bytes 12582912 | tf_op jit(solution)/shard_map/all_gather | solution.py:168
  185.9 683.0 %all-reduce.13.cloned.1.call-start = ((), (), s32[]{:S(2)}) async-start(), calls=%async_computation.12 | async-start | bytes 17825792 | tf_op jit(solution)/shard_map/psum | solution.py:110
  189.5 310.7 %copy-start.27 = (bf16[8,16,2048]{2,1,0:T(8,128)(2,1)S(1)}, bf16[8,16,2048]{2,1,0:T(8,128)(2,1)}, u32[]{:S(2)}) copy-start(bf16[8,16,2048]{2,1,0:T(8,128)(2,1)} %param.35) | copy-start | bytes 1572868
  500.3 6.3 copy-start.22
  507.6 5.5 copy-start.26
  514.4 17.7 copy-start.34
  532.1 16.4 slice-start.6
  537.0 11.6 slice-start.7
  559.7 443.9 %reduce-scatter.3.cloned.1.call-start = ((), (), s32[]{:S(2)}) async-start(), calls=%async_computation.8 | async-start | bytes 10485760 | tf_op jit(solution)/shard_map/reduce_scatter | solution.py:287
  901.5 11.8 copy-start.17
  918.2 174.7 %reduce-scatter.5.cloned.1.call-start = ((), (), s32[]{:S(2)}) async-start(), calls=%async_computation.9 | async-start | bytes 10485760 | tf_op jit(solution)/shard_map/reduce_scatter | solution.py:288
  929.1 782.5 %all-reduce.11.cloned.1.call-start = ((), (), s32[]{:S(2)}) async-start(), calls=%async_computation.11 | async-start | bytes 35651584 | tf_op jit(solution)/shard_map/psum | solution.py:110
  930.1 19.4 %slice-start.4 = ((s8[8388608]{0:T(1024)(128)(4,1)}), s8[4194304]{0:T(1024)(128)(4,1)S(1)}, s32[]{:S(2)}) async-start(s8[8388608]{0:T(1024)(128)(4,1)} %bitcast.208), calls=%async_computation.18 | async-start | bytes 8388608
  934.6 14.9 slice-start.5
  934.6 15.0 copy-start.14
  953.1 146.5 %copy-start.21 = (bf16[16,8,3,512]{3,1,2,0:T(8,128)(2,1)S(1)}, bf16[16,8,3,512]{3,1,2,0:T(8,128)(2,1)}, u32[]{:S(2)}) copy-start(bf16[16,8,3,512]{3,1,2,0:T(8,128)(2,1)} %copy-done.20) | copy-start | bytes 1179652
  1115.1 721.6 %all-reduce.9.cloned.1.call-start = ((), (), s32[]{:S(2)}) async-start(), calls=%async_computation.10 | async-start | bytes 15204352 | tf_op jit(solution)/shard_map/psum | solution.py:318
  1120.7 9.9 copy-start.23
  1125.2 7.2 copy-start.25
  1126.3 585.3 %copy-start.42 = (f32[4,128]{1,0:T(4,128)S(1)}, f32[4,128]{1,0:T(4,128)}, u32[]{:S(2)}) copy-start(f32[4,128]{1,0:T(4,128)} %copy-done.40) | copy-start | bytes 6148
  1719.0 15.2 slice-start
  1719.0 9.3 copy-start.4
  1719.0 15.1 slice-start.1
  1728.4 13.0 slice-start.2
  1734.2 7.2 copy-start.7
  1734.2 7.2 slice-start.3
  1734.2 7.1 copy-start.44
  1741.4 109.3 %copy-start.1 = (bf16[8,16,2048]{2,1,0:T(8,128)(2,1)S(1)}, bf16[8,16,2048]{2,1,0:T(8,128)(2,1)}, u32[]{:S(2)}) copy-start(bf16[8,16,2048]{2,1,0:T(8,128)(2,1)} %param.37) | copy-start | bytes 1572868
  1836.7 11.1 copy-start.33
  1836.7 12.0 copy-start.32
  1836.7 13.0 copy-start.31
  (26 other events, 77.8 us)
Sparse Core Ops, SparseCore 0:
  12.1 19.4 all-gather.6
  44.1 53.7 all-gather.8
  100.3 52.4 all-gather.10
  154.2 10.5 all-gather.12
  166.1 21.0 all-gather.16
  190.2 308.9 all-reduce.14
  500.7 18.8 all-gather.14
  559.9 308.9 all-reduce.12
  918.3 85.2 reduce-scatter.2
  1006.6 86.3 reduce-scatter.4
  1115.2 596.3 all-reduce.10
  1719.1 117.4 all-reduce.8
where the time goes:
time: 1870 us; the launch traced here: 1860 us
  waiting for transfers between devices  1510 us (81%)
  matrix products  227 us (12%)
  local copies, waits for them, and re-layouts  58 us (3%)
  other arithmetic  44.6 us (2%)
    psum x3, waiting for transfers between devices, reduce_heads(): return lax.psum((partials[0], partials[1]), 'tp')  1180 us
    psum x1, waiting for transfers between devices, body(): lax.psum((adapter_terms[0], adapter_terms[1], adapter_terms[2], adapter_t...  88.1 us
    reduce_scatter x1, waiting for transfers between devices, body(): lax.psum_scatter(grad_valrows, 'ctx', scatter_dimension=1, tiled=True)  86.9 us
    dot_general x12, matrix products, matmul_nt(): lax.dot_general(left_mat, right_mat, (((1,), (1,)), ((), ())), preferred_...  81.3 us
    dot_general x12, matrix products, matmul(): return jnp.dot(left_mat, right_mat, preferred_element_type=jnp.float32)  72.6 us
    reduce_scatter x1, waiting for transfers between devices, body(): lax.psum_scatter(grad_keyrows, 'ctx', scatter_dimension=1, tiled=True)  49.3 us
    all_gather x1, waiting for transfers between devices, body(): lax.all_gather(key_rows, 'ctx', axis=1, tiled=True)  48.5 us
    all_gather x1, waiting for transfers between devices, body(): lax.all_gather(value_rows, 'ctx', axis=1, tiled=True)  43.8 us
  transfers between devices with their start and end apart: 12, of which 10 were waited for; matrix products, arithmetic and copies ran while one was open for 9% of the time, Pallas kernels for 0%

commit v1 on v0

--- a/solution.py
+++ b/solution.py
@@ -6,6 +6,32 @@
 HD = 128
 PIC = 256
 NORM_EPS = 1e-05
+
+
+def replace_the_packet(sample, which_dim):
+    prior = list(sample.shape[1:])
+    prior[which_dim] *= sample.shape[0]
+    response = jnp.moveaxis(sample, 0, which_dim).reshape(prior)
+    return response
+
+
+def try_all_tiles(buf, mesh_dim):
+    q_n = jax.lax.axis_size(mesh_dim)
+    block_now = buf[None]
+    for jj in range(q_n.bit_length() - 1):
+        last = 1 << jj
+        vec_out = jax.lax.ppermute(
+            block_now, axis_name=mesh_dim, perm=tuple(((d, d ^ last) for d in range(q_n)))
+        )
+        m_next = jnp.stack([block_now, vec_out])
+        y2 = jax.lax.axis_index(mesh_dim) >> jj & 1
+        block_now = jnp.where(y2 == 0, m_next, m_next[::-1]).reshape(-1, *buf.shape)
+    return block_now
+
+
+def fill_rings_for(values, original, at_axis):
+    b_next = replace_the_packet(try_all_tiles(values, original), at_axis)
+    return b_next
 
 
 def layer_norm(inputs, gains, biases):
@@ -185,7 +211,7 @@
     value_rows = projected[:, 2 * local_width :].reshape(seq_here, local_len, local_width)
     pieces = (
         lax.all_gather(key_rows, "ctx", axis=1, tiled=True),
-        lax.all_gather(value_rows, "ctx", axis=1, tiled=True),
+        fill_rings_for(value_rows, "ctx", 1),
     )
     piece_len = pieces[0].shape[1]
     key_pos = jnp.arange(piece_len, dtype=jnp.int32)

time: 1870 us -> 1890 us (1.011)
    ppermute x0 -> x2, waiting for transfers between devices: none -> 92.3 us  [try_all_tiles(): jax.lax.ppermute(block_now, axis_name=mesh_dim, perm=tuple(((d, d ^ last)...]
    all_gather x1, waiting for transfers between devices: 48.5 us -> 0.01 us  [body(): lax.all_gather(key_rows, 'ctx', axis=1, tiled=True)]
    reduce_scatter x1, waiting for transfers between devices: 86.9 us -> 47.1 us  [body(): lax.psum_scatter(grad_valrows, 'ctx', scatter_dimension=1, tiled=True)]
    reduce_scatter x1, waiting for transfers between devices: 49.3 us -> 86.9 us  [body(): lax.psum_scatter(grad_keyrows, 'ctx', scatter_dimension=1, tiled=True)]
    all_gather x1, waiting for transfers between devices: 43.8 us -> 9.73 us  [body(): lax.all_gather(value_rows, 'ctx', axis=1, tiled=True)]
  transfers between devices with their start and end apart: 12 -> 14, of which waited for: 10 -> 11; matrix products, arithmetic and copies ran while one was open for 9% -> 13% of each run, Pallas kernels for 0% -> 0%
where the time goes in v1:
time: 1890 us; the launch traced here: 1880 us
  waiting for transfers between devices  1510 us (80%)
  matrix products  227 us (12%)
  local copies, waits for them, and re-layouts  71 us (4%)
  other arithmetic  56.2 us (3%)
    psum x3, waiting for transfers between devices, reduce_heads(): return lax.psum((partials[0], partials[1]), 'tp')  1170 us
    ppermute x2, waiting for transfers between devices, try_all_tiles(): jax.lax.ppermute(block_now, axis_name=mesh_dim, perm=tuple(((d, d ^ last)...  92.3 us
    psum x1, waiting for transfers between devices, body(): lax.psum((adapter_terms[0], adapter_terms[1], adapter_terms[2], adapter_t...  88.2 us
    reduce_scatter x1, waiting for transfers between devices, body(): lax.psum_scatter(grad_keyrows, 'ctx', scatter_dimension=1, tiled=True)  86.9 us
    dot_general x12, matrix products, matmul_nt(): lax.dot_general(left_mat, right_mat, (((1,), (1,)), ((), ())), preferred_...  80.5 us
    dot_general x12, matrix products, matmul(): return jnp.dot(left_mat, right_mat, preferred_element_type=jnp.float32)  72.2 us
    reduce_scatter x1, waiting for transfers between devices, body(): lax.psum_scatter(grad_valrows, 'ctx', scatter_dimension=1, tiled=True)  47.1 us
  transfers between devices with their start and end apart: 14, of which 11 were waited for; matrix products, arithmetic and copies ran while one was open for 13% of the time, Pallas kernels for 0%

profile of v1, /device:TPU:0, one launch (start us, length us, event | category | flops | bytes accessed | tf_op | source)
XLA Modules:
  0.0 1884.2 jit_solution(2002894273677613180)
XLA Ops:
  7.3 4.7 copy.69
  12.6 3.2 convert_reduce_fusion
  23.4 8.2 all-gather.7.cloned.1.call-done
  31.6 10.1 fusion.56
  49.9 35.0 %collective-permute-done = bf16[1,4,256,512]{3,2,1,0:T(8,128)(2,1)} collective-permute-done((bf16[1,4,256,512]{3,2,1,0:T(8,128)(2,1)S(1)}, bf16[1,4,256,512]{3,2,1,0:T(8,128)(2,1)}, u32[]{:S(2)}, u32[]{:S(2)}) %collective-permute-start) | collective-permute-done | bytes 1048608 | tf_op jit(solution)/shard_map/ppermute | solution.py:23
  98.4 57.3 %collective-permute-done.1 = bf16[2,4,256,512]{3,2,1,0:T(8,128)(2,1)} collective-permute-done((bf16[2,4,256,512]{3,2,1,0:T(8,128)(2,1)}, bf16[2,4,256,512]{3,2,1,0:T(8,128)(2,1)}, u32[]{:S(2)}, u32[]{:S(2)}) %collective-permute-start.1) | collective-permute-done | bytes 2097184 | tf_op jit(solution)/shard_map/ppermute | solution.py:23
  155.7 3.2 pad_maximum_fusion
  161.9 7.5 copy.71
  169.4 7.7 reshape_reshape.6
  177.1 12.7 fusion.53
  189.9 10.6 fusion.54
  203.3 7.2 fusion.36
  211.6 3.4 fusion.32
  215.1 15.4 fusion.60
  230.5 288.3 %all-reduce.15.cloned.1.call-done = (f32[1024,2048]{1,0:T(8,128)}, f32[1024,128]{1,0:T(8,128)}) async-done(((f32[1024,2048]{1,0:T(8,128)}, f32[1024,128]{1,0:T(8,128)}), (f32[1024,2048]{1,0:T(8,128)}, f32[1024,128]{1,0:T(8,128)})) %all-reduce.15.cloned.1.call-update) | async-done | bytes 8912912 | tf_op jit(solution)/shard_map/psum | solution.py:136
  519.8 6.3 fusion.55
  534.0 5.0 all-gather.13.cloned.1.call-done
  539.0 12.5 fusion.57
  551.5 4.9 multiply_convert_fusion.1
  556.4 9.4 fusion.3
  567.9 11.0 fusion.61
  580.4 307.7 %all-reduce.13.cloned.1.call-done = (f32[1024,2048]{1,0:T(8,128)}, f32[1024,128]{1,0:T(8,128)}) async-done(((f32[1024,2048]{1,0:T(8,128)}, f32[1024,128]{1,0:T(8,128)}), (f32[1024,2048]{1,0:T(8,128)}, f32[1024,128]{1,0:T(8,128)})) %all-reduce.13.cloned.1.call-update) | async-done | bytes 8912912 | tf_op jit(solution)/shard_map/psum | solution.py:136
  889.2 7.4 multiply_reduce_fusion
  896.7 5.4 fusion.50
  902.8 3.7 fusion.16
  906.7 3.4 fusion.33
  910.2 5.2 fusion.63
  919.6 10.7 fusion.21
  932.2 9.7 all-gather.17.cloned.1.call-done
  941.9 8.7 multiply_convert_fusion
  950.7 3.4 copy-done.9
  954.1 4.9 multiply_bitcast_fusion
  960.0 4.6 fusion.59
  964.7 14.8 fusion.58
  979.5 2.9 fusion.29
  984.3 47.1 %reduce-scatter.5.cloned.1.call-done = f32[4,256,4,128]{1,3,2,0:T(8,128)} async-done(((f32[4,1024,4,128]{1,3,2,0:T(8,128)}), f32[4,256,4,128]{1,3,2,0:T(8,128)}) %reduce-scatter.5.cloned.1.call-update) | async-done | bytes 2097168 | tf_op jit(solution)/shard_map/reduce_scatter | solution.py:314
  1033.8 86.9 %reduce-scatter.3.cloned.1.call-done = f32[4,256,4,128]{1,3,2,0:T(8,128)} async-done(((f32[4,1024,4,128]{1,3,2,0:T(8,128)}), f32[4,256,4,128]{1,3,2,0:T(8,128)}) %reduce-scatter.3.cloned.1.call-update) | async-done | bytes 2097168 | tf_op jit(solution)/shard_map/reduce_scatter | solution.py:313
  1127.4 12.4 fusion.64
  1143.4 3.9 fusion.69
  1147.4 4.3 fusion.70
  1152.9 4.2 fusion.67
  1163.0 575.1 %all-reduce.11.cloned.1.call-done = (f32[1024,2048]{1,0:T(8,128)}, f32[1024,128]{1,0:T(8,128)}, f32[1024,2048]{1,0:T(8,128)}, f32[1024,128]{1,0:T(8,128)}) async-done(((f32[1024,2048]{1,0:T(8,128)}, f32[1024,128]{1,0:T(8,128)}, f32[1024,2048]{1,0:T(8,128)}, f32[1024,128]{1,0:T(8,128)}), (f32[1024,2048]{1,0:T(8,128)}, f32[1024,128]{1,0:T(8,128)}, f32[1024,2048]{1,0:T(8,128)}, ...) | async-done | bytes 17825808 | tf_op jit(solution)/shard_map/psum | solution.py:136
  1739.7 4.0 convolution_bitcast_fusion
  1745.5 8.5 fusion.10
  1754.8 5.8 fusion.49
  1760.7 7.1 add_convert_fusion.1
  1767.8 7.2 add_convert_fusion
  1775.0 88.2 %all-reduce.9.cloned.1.call-done = (f32[8,2048,16]{1,2,0:T(8,128)}, f32[8,16,3,512]{3,2,1,0:T(4,128)}, f32[8,512,16]{1,2,0:T(8,128)}, f32[8,16,2048]{2,1,0:T(8,1...) async-done(((f32[8,2048,16]{1,2,0:T(8,128)}, f32[8,16,3,512]{3,2,1,0:T(4,128)}, ...) | async-done | bytes 7340048 | tf_op jit(solution)/shard_map/psum | solution.py:344
  (245 shorter events, 97.9 us)
Async XLA Ops:
  7.2 544.3 %copy-start = (bf16[8,16,2048]{2,1,0:T(8,128)(2,1)S(1)}, bf16[8,16,2048]{2,1,0:T(8,128)(2,1)}, u32[]{:S(2)}) copy-start(bf16[8,16,2048]{2,1,0:T(8,128)(2,1)} %param.37) | copy-start | bytes 1572868
  7.2 11.1 copy-start.51
  7.2 11.1 copy-start.57
  7.2 24.4 %all-gather.7.cloned.1.call-start = ((), (), s32[]{:S(2)}) async-start(), calls=%async_computation.2 | async-start | bytes 9437184 | tf_op jit(solution)/shard_map/all_gather | solution.py:193
  12.0 165.1 %all-gather.9.cloned.1.call-start = ((), (), s32[]{:S(2)}) async-start(), calls=%async_computation.3 | async-start | bytes 5242880 | tf_op jit(solution)/shard_map/all_gather | solution.py:213
  12.5 29.2 %copy-start.21 = (bf16[16,8,3,512]{3,1,2,0:T(8,128)(2,1)}, bf16[16,8,3,512]{3,1,2,0:T(8,128)(2,1)S(1)}, u32[]{:S(2)}) copy-start(bf16[16,8,3,512]{3,1,2,0:T(8,128)(2,1)S(1)} %copy.94) | copy-start | bytes 1179652
  12.6 9.5 copy-start.30
  23.4 18.3 copy-start.25
  46.3 44.4 %copy-start.56 = (s32[4,2]{0,1:T(2,128)S(1)}, s32[4,2]{0,1:T(2,128)}, u32[]{:S(2)}) copy-start(s32[4,2]{0,1:T(2,128)} %param.22) | copy-start | bytes 100
  46.3 157.0 %all-gather.11.cloned.1.call-start = ((), (), s32[]{:S(2)}) async-start(), calls=%async_computation.4 | async-start | bytes 3145728 | tf_op jit(solution)/shard_map/all_gather | solution.py:199
  47.0 168.1 %all-gather.15.cloned.1.call-start = ((), (), s32[]{:S(2)}) async-start(), calls=%async_computation.6 | async-start | bytes 12582912 | tf_op jit(solution)/shard_map/all_gather | solution.py:200
  47.6 471.1 %all-reduce.15.cloned.1.call-start = ((), (), s32[]{:S(2)}) async-start(), calls=%async_computation.13 | async-start | bytes 17825792 | tf_op jit(solution)/shard_map/psum | solution.py:136
  48.1 36.7 %collective-permute-start = (bf16[1,4,256,512]{3,2,1,0:T(8,128)(2,1)S(1)}, bf16[1,4,256,512]{3,2,1,0:T(8,128)(2,1)}, u32[]{:S(2)}, u32[]{:S(2)}) collective-permute-start(bf16[1,4,256,512]{3,2,1,0:T(8,128)(2,1)S(1)} %bitcast.231), channel_id=1, source_target_pairs={{0,4},{4,0},{8,12},{12,8},{1,5},{5,1},{9,13},{13,9},{2,6},{6,2},{1... | collective-permute-start | bytes 3145736 | tf_op jit(solution)/shard_map/ppermute | solution.py:23
  88.9 66.8 %collective-permute-start.1 = (bf16[2,4,256,512]{3,2,1,0:T(8,128)(2,1)}, bf16[2,4,256,512]{3,2,1,0:T(8,128)(2,1)}, u32[]{:S(2)}, u32[]{:S(2)}) collective-permute-start(bf16[2,4,256,512]{3,2,1,0:T(8,128)(2,1)} %get-tuple-element.52), channel_id=1, source_target_pairs={{0,8},{4,12},{8,0},{12,4},{1,9},{5,13},{9,1},{13,5},{2,10},{6,14},... | collective-permute-start | bytes 6291464 | tf_op jit(solution)/shard_map/ppermute | solution.py:23
  98.4 78.8 %copy-start.17 = (bf16[4,256,4,128]{1,3,2,0:T(8,128)(2,1)}, bf16[4,256,4,128]{1,3,2,0:T(8,128)(2,1)S(1)}, u32[]{:S(2)}) copy-start(bf16[4,256,4,128]{1,3,2,0:T(8,128)(2,1)S(1)} %copy.83) | copy-start | bytes 3145732
  177.1 12.7 copy-start.12
  189.9 12.2 copy-start.40
  202.1 8.5 copy-start.19
  210.6 328.4 %all-gather.13.cloned.1.call-start = ((), (), s32[]{:S(2)}) async-start(), calls=%async_computation.5 | async-start | bytes 12582912 | tf_op jit(solution)/shard_map/all_gather | solution.py:194
  211.2 676.9 %all-reduce.13.cloned.1.call-start = ((), (), s32[]{:S(2)}) async-start(), calls=%async_computation.12 | async-start | bytes 17825792 | tf_op jit(solution)/shard_map/psum | solution.py:136
  215.1 303.7 %copy-start.43 = (f32[4,128]{1,0:T(4,128)S(1)}, f32[4,128]{1,0:T(4,128)}, u32[]{:S(2)}) copy-start(f32[4,128]{1,0:T(4,128)} %copy-done.42) | copy-start | bytes 6148
  215.1 304.7 %copy-start.28 = (bf16[8,16,2048]{2,1,0:T(8,128)(2,1)S(1)}, bf16[8,16,2048]{2,1,0:T(8,128)(2,1)}, u32[]{:S(2)}) copy-start(bf16[8,16,2048]{2,1,0:T(8,128)(2,1)} %param.35) | copy-start | bytes 1572868
  526.2 363.0 %copy-start.46 = (f32[1024]{0:T(1024)}, f32[1024]{0:T(1024)S(1)}, u32[]{:S(2)}) copy-start(f32[1024]{0:T(1024)S(1)} %broadcast_multiply_fusion.1) | copy-start | bytes 12292
  534.0 17.5 copy-start.36
  551.5 16.5 slice-start.6
  556.4 11.6 slice-start.7
  579.0 362.9 %all-gather.17.cloned.1.call-start = ((), (), s32[]{:S(2)}) async-start(), calls=%async_computation.7 | async-start | bytes 5242880 | tf_op jit(solution)/shard_map/all_gather | solution.py:293
  580.4 451.0 %reduce-scatter.5.cloned.1.call-start = ((), (), s32[]{:S(2)}) async-start(), calls=%async_computation.9 | async-start | bytes 10485760 | tf_op jit(solution)/shard_map/reduce_scatter | solution.py:314
  889.2 7.5 copy-start.50
  930.2 190.4 %reduce-scatter.3.cloned.1.call-start = ((), (), s32[]{:S(2)}) async-start(), calls=%async_computation.8 | async-start | bytes 10485760 | tf_op jit(solution)/shard_map/reduce_scatter | solution.py:313
  941.9 12.2 copy-start.18
  959.0 779.1 %all-reduce.11.cloned.1.call-start = ((), (), s32[]{:S(2)}) async-start(), calls=%async_computation.11 | async-start | bytes 35651584 | tf_op jit(solution)/shard_map/psum | solution.py:136
  960.0 19.4 %slice-start.4 = ((s8[8388608]{0:T(1024)(128)(4,1)}), s8[4194304]{0:T(1024)(128)(4,1)S(1)}, s32[]{:S(2)}) async-start(s8[8388608]{0:T(1024)(128)(4,1)} %bitcast.220), calls=%async_computation.18 | async-start | bytes 8388608
  964.7 14.8 slice-start.5
  964.7 14.8 copy-start.15
  1127.4 12.4 copy-start.13
  1127.4 12.4 copy-start.22
  1141.6 721.6 %all-reduce.9.cloned.1.call-start = ((), (), s32[]{:S(2)}) async-start(), calls=%async_computation.10 | async-start | bytes 15204352 | tf_op jit(solution)/shard_map/psum | solution.py:344
  1143.4 9.5 copy-start.24
  1152.9 585.2 %copy-start.45 = (f32[4,128]{1,0:T(4,128)S(1)}, f32[4,128]{1,0:T(4,128)}, u32[]{:S(2)}) copy-start(f32[4,128]{1,0:T(4,128)} %copy-done.42) | copy-start | bytes 6148
  1745.5 15.1 slice-start
  1745.5 9.3 copy-start.4
  1745.5 15.1 slice-start.1
  1754.8 13.0 slice-start.2
  1767.8 109.3 %copy-start.1 = (bf16[8,16,2048]{2,1,0:T(8,128)(2,1)S(1)}, bf16[8,16,2048]{2,1,0:T(8,128)(2,1)}, u32[]{:S(2)}) copy-start(bf16[8,16,2048]{2,1,0:T(8,128)(2,1)} %param.37) | copy-start | bytes 1572868
  1863.1 11.1 copy-start.35
  1863.1 12.0 copy-start.34
  1863.1 13.0 copy-start.33
  (34 other events, 129.3 us)
Sparse Core Ops, SparseCore 0:
  12.1 19.4 all-gather.6
  46.4 83.6 all-gather.8
  131.7 10.2 all-gather.10
  143.4 21.0 all-gather.14
  210.7 307.9 all-reduce.14
  520.1 18.8 all-gather.12
  579.1 308.9 all-reduce.12
  890.5 51.4 all-gather.16
  945.0 86.3 reduce-scatter.4
  1034.3 86.3 reduce-scatter.2
  1141.7 596.3 all-reduce.10
  1745.6 117.5 all-reduce.8
